TPU v7x, 32 devices: a whole 2x2x4 slice. The times are simulated.
32 devices in a mesh: occ: 8 (over y, x, core), frag: 4 (over z).
Axes of the slice: x: 2, y: 2, z: 4, core: 2. Of those that a mesh axis runs over, the one named last changes fastest.
Arguments:
- factors: bfloat16 [32, 512, 1280], P(('frag', 'occ')), parts along dimension 0, may hold values from -1 to 1
- occ_energy: float32 [32], P('frag'), parts along dimension 0, may hold values from -2 to -0.3
- vir_energy: float32 [2048], P('frag'), parts along dimension 0, may hold values from 0.2 to 4
- coeffs: bfloat16 [4096, 512], P('frag'), parts along dimension 0, may hold values from -0.25 to 0.25
Outputs:
- back: bfloat16 [1280, 32, 1024], P('occ', 'frag'), parts along dimension 1
There are 4 independent parts, one for each index of `frag`. A program takes and returns all parts, laid end to end along the dimension named above; each array names one. Nothing has to cross between parts.
All inputs are finite; a program needn't handle non-finite values.
Results may differ from a plain program's by a relative error of at most 0.008.
Values may be sent and summed in bfloat16 or wider, within the bound.
A program may use at most 64 MiB of HBM per device.

v0:
```python
import jax
import jax.numpy as jnp
from jax import lax
from jax.experimental import pallas as pl
from jax.experimental.pallas import tpu as pltpu
from jax.sharding import PartitionSpec as P

OFFSETS = 3


def passed_along(block, axis, distance):
    devices = range(lax.axis_size(axis))
    route = [((i - distance) % len(devices), i) for i in devices]
    return lax.ppermute(block, axis, route)


def on_device(factors, occ_energy, vir_energy, coeffs):
    mine = factors[0]
    count = lax.axis_size("occ")
    index = lax.axis_index("occ")
    partners = []
    current = mine
    for offset in range(1, OFFSETS + 1):
        current = passed_along(current, "occ", -1)
        partners.append(current)
    own_energy = lax.dynamic_index_in_dim(occ_energy, index, 0, False)
    own = jnp.zeros((mine.shape[1], mine.shape[0]), jnp.float32)
    outgoing = []
    for offset in range(1, OFFSETS + 1):
        partner = partners[offset - 1]
        other_energy = lax.dynamic_index_in_dim(occ_energy, (index + offset) % count, 0, False)
        kmat = lax.dot_general(
            mine, partner, (((1,), (1,)), ((), ())), preferred_element_type=jnp.float32
        )
        denom = own_energy + other_energy - vir_energy[:, None] - vir_energy[None, :]
        amps = (kmat / denom).astype(jnp.bfloat16)
        own = own + lax.dot_general(
            partner, amps, (((0,), (1,)), ((), ())), preferred_element_type=jnp.float32
        )
        sent = lax.dot_general(
            mine, amps, (((0,), (0,)), ((), ())), preferred_element_type=jnp.float32
        )
        outgoing.append(sent.astype(jnp.bfloat16))
    incoming = jnp.zeros_like(own)
    for offset in range(1, OFFSETS + 1):
        arrived = passed_along(outgoing[offset - 1], "occ", offset)
        incoming = incoming + arrived.astype(jnp.float32)
    gamma = (own + incoming).astype(jnp.bfloat16)[None]
    slabs = lax.all_to_all(gamma, "occ", split_axis=1, concat_axis=0, tiled=True)
    return jnp.einsum("ipa,ma->pim", slabs, coeffs, preferred_element_type=jnp.float32).astype(
        jnp.bfloat16
    )


LANES = 128
ROWS = 128
CHUNK = ROWS // 2
HALVES = 1

NEAR = ((2, 3, 0, 0), (2, 3, 1, 0), (5, 5, 0, 1), (4, 4, 1, 1))
SIDE = ((2, 2, 3), (2, 2, 4), (2, 2, 5), (3, 3, 4), (3, 3, 5), (4, 4, 5))
FAR = ((6, 7, 0, 0), (6, 7, 1, 0), (6, 7, 4, 0), (6, 7, 5, 0), (6, 6, 3, 1), (7, 7, 2, 1))


def flipped(a, b):
    bits = [(a // w % 2 + b // w % 2) % 2 * w for w in (1, 2, 4)]
    return bits[0] + bits[1] + bits[2]


def entry(table, column, n):
    packed = sum(row[column] << (3 * k) for k, row in enumerate(table))
    return lax.shift_right_logical(jnp.int32(packed), jnp.int32(3) * n) % 8


def gathered_kernel(
    mine_ref, energy_ref, vir_ref, out_ref,
    blocks, slabs, total, turned, vcol, held, local_sem, own_sem, fwd_sem, sib_sem, recv_sem,
):
    me = lax.axis_index("occ")
    virtuals, depth = mine_ref.shape
    width = total.shape[1]
    window = turned.shape[0]
    steps = virtuals // ROWS
    chunks = virtuals // CHUNK
    first = me * width
    lead = pl.multiple_of(first // LANES * LANES, LANES)
    skip = pl.multiple_of(first % LANES, 32)

    barrier = pltpu.get_barrier_semaphore()
    for bit in (1, 2, 4):
        pl.semaphore_signal(
            barrier, inc=1, device_id={"occ": flipped(me, bit)},
            device_id_type=pl.DeviceIdType.MESH,
        )
    pl.semaphore_wait(barrier, 3)

    def rows_of(q):
        return pl.ds(pl.multiple_of(q * CHUNK, CHUNK), CHUNK)

    def send(source, label, q, bit, send_sem):
        return pltpu.make_async_remote_copy(
            src_ref=source,
            dst_ref=blocks.at[flipped(me, label), rows_of(q)],
            send_sem=send_sem,
            recv_sem=recv_sem.at[flipped(label, bit), q],
            device_id={"occ": flipped(me, bit)},
            device_id_type=pl.DeviceIdType.MESH,
        )

    def own_send(q, axis):
        return send(mine_ref.at[rows_of(q)], 0, q, 2 + 2 * axis, own_sem.at[axis, q])

    def far_send(q, label):
        return send(
            blocks.at[flipped(me, label), rows_of(q)], label, q, 6 - label, fwd_sem.at[q]
        )

    def sib_send(q, label):
        source = mine_ref.at[rows_of(q)] if label == 0 else blocks.at[flipped(me, label), rows_of(q)]
        return send(source, label, q, 1, sib_sem.at[label // 2, q])

    def arrived(label, q):
        place = blocks.at[flipped(me, label), rows_of(q)]
        pltpu.make_async_copy(place, place, recv_sem.at[label, q]).wait()

    @pl.loop(0, chunks)
    def _(q):
        own_send(q, 0).start()
        own_send(q, 1).start()
        sib_send(q, 0).start()

    local = pltpu.make_async_copy(mine_ref, blocks.at[me], local_sem)
    local.start()
    total[...] = jnp.zeros_like(total)
    held[...] = jnp.zeros_like(held)
    slabs[...] = jnp.zeros_like(slabs)
    for t in range(steps):
        part = vir_ref[:, t * ROWS:(t + 1) * ROWS]
        vcol[t * ROWS:(t + 1) * ROWS, :] = jnp.broadcast_to(part, (ROWS, ROWS)).T
    local.wait()

    def turn(label, t):
        u = flipped(me, label)
        rows = pl.ds(pl.multiple_of(t * ROWS, ROWS), ROWS)
        turned[...] = blocks[u, rows, pl.ds(lead, window)].astype(jnp.float32).T
        slabs[u, :, rows] = turned[pl.ds(skip, width), :].astype(jnp.bfloat16)

    def rows_at(t):
        return pl.ds(pl.multiple_of(t * ROWS, ROWS), ROWS)

    def gather(item):
        ua, ta, ub, tb, v = item
        left = jnp.concatenate([slabs[ua, :, rows_at(ta)], slabs[ub, :, rows_at(tb)]], axis=1)
        both = jnp.dot(slabs[v], held[...], preferred_element_type=jnp.float32)
        other = lax.dot_general(
            left, held[...], (((1,), (1,)), ((), ())), preferred_element_type=jnp.float32
        )
        total[ua, :, rows_at(ta)] += both[:, :ROWS]
        total[ub, :, rows_at(tb)] += both[:, ROWS:]
        total[v] += other

    def step(item, before):
        ua, ta, ub, tb, v = item = (flipped(me, item[0]), item[1], flipped(me, item[2]), item[3], flipped(me, item[4]))
        some = jnp.concatenate([blocks[ua, rows_at(ta), :], blocks[ub, rows_at(tb), :]], axis=0)
        level = jnp.concatenate(
            [energy_ref[ua] - vir_ref[:, rows_at(ta)], energy_ref[ub] - vir_ref[:, rows_at(tb)]],
            axis=1,
        ) + energy_ref[v]
        fresh = []
        for h in range(HALVES):
            rows = slice(h * (virtuals // HALVES), (h + 1) * (virtuals // HALVES))
            kmat = lax.dot_general(
                blocks[v, rows, :], some, (((1,), (1,)), ((), ())),
                preferred_element_type=jnp.float32,
            )
            denom = level - vcol[rows, 0:1]
            fresh.append((kmat / denom).astype(jnp.bfloat16))
        gather(before)
        for h in range(HALVES):
            held[h * (virtuals // HALVES):(h + 1) * (virtuals // HALVES), :] = fresh[h]
        return item

    @pl.loop(0, chunks)
    def _(q):
        arrived(1, q)

    @pl.loop(0, steps)
    def _(t):
        turn(0, t)
        turn(1, t)

    def first_pair(s, before):
        return step((1, 2 * s, 1, 2 * s + 1, 0), before)

    start = (flipped(me, 1), jnp.int32(0), flipped(me, 1), jnp.int32(1), me)
    before = lax.fori_loop(0, steps // 2, first_pair, start)

    def item_of(table, n, t):
        return (
            entry(table, 0, n), t - entry(table, 3, n), entry(table, 1, n), t, entry(table, 2, n)
        )

    def near(t, before):
        for k in (0, 1):
            q = 2 * t + k
            arrived(2, q)
            sib_send(q, 2).start()
            if k == 0:
                far_send(q, 2).start()
            arrived(4, q)
            sib_send(q, 4).start()
            if k == 1:
                far_send(q, 4).start()
        turn(2, t)
        turn(4, t)
        for k in (0, 1):
            arrived(3, 2 * t + k)
            arrived(5, 2 * t + k)
        turn(3, t)
        turn(5, t)
        count = 2 + 2 * (t % 2)
        return lax.fori_loop(0, count, lambda n, c: step(item_of(NEAR, n, t), c), before)

    before = lax.fori_loop(0, steps, near, before)

    def far(t, before):
        def side(n, c):
            m = t // 2 * 3 + n
            s = t % 2
            u = entry(SIDE, 0, m)
            return step((u, 2 * s, u, 2 * s + 1, entry(SIDE, 2, m)), c)

        before = lax.fori_loop(0, len(SIDE) // 2, side, before)
        for k in (0, 1):
            q = 2 * t + k
            arrived(6, q)
            sib_send(q, 6).start()
        turn(6, t)
        for k in (0, 1):
            arrived(7, 2 * t + k)
        turn(7, t)
        count = 4 + 2 * (t % 2)
        return lax.fori_loop(0, count, lambda n, c: step(item_of(FAR, n, t), c), before)

    before = lax.fori_loop(0, steps, far, before)

    def last_pair(s, before):
        return step((7, 2 * s, 7, 2 * s + 1, 6), before)

    gather(lax.fori_loop(0, steps // 2, last_pair, before))

    @pl.loop(0, 2 * OFFSETS + 2)
    def _(u):
        out_ref[u] = total[u].astype(jnp.bfloat16)

    @pl.loop(0, steps)
    def _(t):
        for k in (0, 1):
            q = 2 * t + k
            own_send(q, 0).wait_send()
            own_send(q, 1).wait_send()
            for label in (0, 2, 4, 6):
                sib_send(q, label).wait_send()
            far_send(q, 2 if k == 0 else 4).wait_send()


def gathered(factors, occ_energy, vir_energy, coeffs):
    _, virtuals, depth = factors.shape
    count = lax.axis_size("occ")
    width = depth // count
    window = max(
        -(-(d * width % LANES + width) // LANES) * LANES for d in range(count)
    )
    steps = virtuals // ROWS
    chunks = virtuals // CHUNK
    pair_flops = 2 * virtuals * virtuals * (depth + 2 * width)
    gamma = pl.pallas_call(
        gathered_kernel,
        out_shape=jax.ShapeDtypeStruct((count, width, virtuals), jnp.bfloat16),
        in_specs=[
            pl.BlockSpec(memory_space=pl.ANY),
            pl.BlockSpec(memory_space=pltpu.SMEM),
            pl.BlockSpec(memory_space=pltpu.VMEM),
        ],
        out_specs=pl.BlockSpec(memory_space=pltpu.VMEM),
        scratch_shapes=[
            pltpu.VMEM((count, virtuals, depth), jnp.bfloat16),
            pltpu.VMEM((count, width, virtuals), jnp.bfloat16),
            pltpu.VMEM((count, width, virtuals), jnp.float32),
            pltpu.VMEM((window, ROWS), jnp.float32),
            pltpu.VMEM((virtuals, ROWS), jnp.float32),
            pltpu.VMEM((virtuals, 2 * ROWS), jnp.bfloat16),
            pltpu.SemaphoreType.DMA,
            pltpu.SemaphoreType.DMA((2, chunks)),
            pltpu.SemaphoreType.DMA((chunks,)),
            pltpu.SemaphoreType.DMA((4, chunks)),
            pltpu.SemaphoreType.DMA((8, chunks)),
        ],
        compiler_params=pltpu.CompilerParams(
            collective_id=0, has_side_effects=True, vmem_limit_bytes=44 * 1024 * 1024
        ),
        cost_estimate=pl.CostEstimate(
            flops=count * OFFSETS * pair_flops, bytes_accessed=count * virtuals * depth * 2,
            transcendentals=0,
        ),
    )(factors[0], occ_energy, vir_energy[None])
    return jnp.einsum("ipa,ma->pim", gamma, coeffs, preferred_element_type=jnp.float32).astype(
        jnp.bfloat16
    )


def fits(count, virtuals, depth):
    width = depth // count
    return (
        count == 8
        and count == 2 * OFFSETS + 2
        and virtuals == 4 * ROWS
        and depth % (LANES * 2) == 0
        and width % 32 == 0
    )


def either(factors, occ_energy, vir_energy, coeffs):
    if fits(lax.axis_size("occ"), factors.shape[1], factors.shape[2]):
        return gathered(factors, occ_energy, vir_energy, coeffs)
    return on_device(factors, occ_energy, vir_energy, coeffs)


def solution(mesh):
    return jax.shard_map(
        either,
        mesh=mesh,
        in_specs=(P(("frag", "occ"), None, None), P("frag"), P("frag"), P("frag", None)),
        out_specs=P("occ", "frag", None),
        check_vma=False,
    )
```

profile of v0, /device:TPU:1, one launch (start us, length us, event | category | flops | bytes accessed | tf_op | source)
XLA Modules:
  0.0 78.0 jit_solution(10685906937087990743)
XLA Ops:
  0.0 0.0 copy-start
  0.0 0.0 copy-start.1
  0.0 1.4 %copy-done.1 = bf16[1,512,1280]{2,1,0:T(8,128)(2,1)S(1)} copy-done((bf16[1,512,1280]{2,1,0:T(8,128)(2,1)S(1)}, bf16[1,512,1280]{2,1,0:T(8,128)(2,1)}, u32[]{:S(2)}) %copy-start.1) | copy-done | bytes 1310744
  1.4 0.0 copy-start.2
  1.4 0.7 copy-done.2
  2.1 0.0 copy-start.3
  2.1 0.7 copy-done.3
  2.7 70.8 %shard_map.46 = bf16[8,160,512]{2,1,0:T(8,128)(2,1)S(1)} custom-call(bf16[512,1280]{1,0:T(8,128)(2,1)S(1)} %bitcast.8, f32[8]{0:T(128)S(1)} %copy-done.3, f32[1,512]{1,0:T(1,128)S(1)} %bitcast.9), custom_call_target="tpu_custom_call" | custom-call | flops 20132659200 | bytes 10485760 | tf_op jit(solution)/shard_map/pallas_call | solution.py:277
  73.5 0.0 copy-done
  73.5 1.6 %convert_bitcast_fusion = bf16[160,8,1024]{2,0,1:T(8,128)(2,1)S(1)} fusion(bf16[8,160,512]{2,1,0:T(8,128)(2,1)S(1)} %shard_map.46, bf16[1024,512]{1,0:T(8,128)(2,1)S(1)} %copy-done), kind=kOutput, calls=%fused_computation | convolution fusion | flops 1343488000 | bytes 4980736 | tf_op jit(solution)/shard_map/ipa,ma->pim/dot_general | solution.py:307
  75.1 2.9 %copy.5 = bf16[160,8,1024]{2,1,0:T(8,128)(2,1)} copy(bf16[160,8,1024]{2,0,1:T(8,128)(2,1)S(1)} %convert_bitcast_fusion) | data formatting | bytes 5242880 | tf_op jit(solution)/shard_map/convert_element_type | solution.py:307
Async XLA Ops:
  0.0 73.5 %copy-start = (bf16[1024,512]{1,0:T(8,128)(2,1)S(1)}, bf16[1024,512]{1,0:T(8,128)(2,1)}, u32[]{:S(2)}) copy-start(bf16[1024,512]{1,0:T(8,128)(2,1)} %param.7) | copy-start | bytes 3145732
  0.0 1.4 %copy-start.1 = (bf16[1,512,1280]{2,1,0:T(8,128)(2,1)S(1)}, bf16[1,512,1280]{2,1,0:T(8,128)(2,1)}, u32[]{:S(2)}) copy-start(bf16[1,512,1280]{2,1,0:T(8,128)(2,1)} %param.4) | copy-start | bytes 3932164
  1.4 0.7 copy-start.2
  2.1 0.7 copy-start.3
where the time goes:
time: 78.2 us; the launch traced here: 78 us
  Pallas kernels  70.8 us (91%)
  local copies, waits for them, and re-layouts  5.67 us (7%)
  matrix products  1.55 us (2%)
    pallas_call x1, Pallas kernels, gathered(): pl.pallas_call(gathered_kernel, out_shape=jax.ShapeDtypeStruct((count, wi...  70.8 us
    convert_element_type x1, local copies, waits for them, and re-layouts, gathered(): jnp.einsum('ipa,ma->pim', gamma, coeffs, preferred_element_type=jnp.float32)  2.93 us
    unnamed x8, local copies, waits for them, and re-layouts  2.74 us

commit v1 on v0

v1 whole, which is shorter than its diff:
```python
import jax
import jax.numpy as jnp
from jax import lax
from jax.experimental import pallas as pl
from jax.experimental.pallas import tpu as pltpu
from jax.sharding import PartitionSpec as P

OFFSETS = 3


def passed_along(block, axis, distance):
    devices = range(lax.axis_size(axis))
    route = [((i - distance) % len(devices), i) for i in devices]
    return lax.ppermute(block, axis, route)


def on_device(factors, occ_energy, vir_energy, coeffs):
    mine = factors[0]
    count = lax.axis_size("occ")
    index = lax.axis_index("occ")
    partners = []
    current = mine
    for offset in range(1, OFFSETS + 1):
        current = passed_along(current, "occ", -1)
        partners.append(current)
    own_energy = lax.dynamic_index_in_dim(occ_energy, index, 0, False)
    own = jnp.zeros((mine.shape[1], mine.shape[0]), jnp.float32)
    outgoing = []
    for offset in range(1, OFFSETS + 1):
        partner = partners[offset - 1]
        other_energy = lax.dynamic_index_in_dim(occ_energy, (index + offset) % count, 0, False)
        kmat = lax.dot_general(
            mine, partner, (((1,), (1,)), ((), ())), preferred_element_type=jnp.float32
        )
        denom = own_energy + other_energy - vir_energy[:, None] - vir_energy[None, :]
        amps = (kmat / denom).astype(jnp.bfloat16)
        own = own + lax.dot_general(
            partner, amps, (((0,), (1,)), ((), ())), preferred_element_type=jnp.float32
        )
        sent = lax.dot_general(
            mine, amps, (((0,), (0,)), ((), ())), preferred_element_type=jnp.float32
        )
        outgoing.append(sent.astype(jnp.bfloat16))
    incoming = jnp.zeros_like(own)
    for offset in range(1, OFFSETS + 1):
        arrived = passed_along(outgoing[offset - 1], "occ", offset)
        incoming = incoming + arrived.astype(jnp.float32)
    gamma = (own + incoming).astype(jnp.bfloat16)[None]
    slabs = lax.all_to_all(gamma, "occ", split_axis=1, concat_axis=0, tiled=True)
    return jnp.einsum("ipa,ma->pim", slabs, coeffs, preferred_element_type=jnp.float32).astype(
        jnp.bfloat16
    )


LANES = 128
ROWS = 128
CHUNK = ROWS // 2

LAG = 3
DEPTH = 2

SIDE = ((2, 0, 4), (2, 2, 4), (2, 0, 5), (2, 2, 5))


def flipped(a, b):
    bits = [(a // w % 2 + b // w % 2) % 2 * w for w in (1, 2, 4)]
    return bits[0] + bits[1] + bits[2]


def entry(table, column, n):
    packed = sum(row[column] << (3 * k) for k, row in enumerate(table))
    return lax.shift_right_logical(jnp.int32(packed), jnp.int32(3) * n) % 8


def gathered_kernel(
    mine_ref, energy_hbm, vir_hbm, out_ref,
    blocks, slabs, total, wide, pick, vcol, held_a, held_b, energy_ref, vir_ref,
    local_sem, small_sem, own_sem, fwd_sem, sib_sem, recv_sem, give_sem, take_sem,
):
    me = lax.axis_index("occ")
    parity = me % 2
    count = blocks.shape[0]
    virtuals, depth = mine_ref.shape
    width = total.shape[1]
    window = pick.shape[1]
    steps = virtuals // ROWS
    chunks = virtuals // CHUNK
    half = virtuals // 2
    first = me * width
    lead = pl.multiple_of(first // LANES * LANES, LANES)
    skip = first % LANES

    def rows_of(q):
        return pl.ds(pl.multiple_of(q * CHUNK, CHUNK), CHUNK)

    def local(q):
        return pltpu.make_async_copy(
            mine_ref.at[rows_of(q)], blocks.at[me, rows_of(q)], local_sem.at[q]
        )

    energy_copy = pltpu.make_async_copy(energy_hbm, energy_ref, small_sem.at[0])
    vir_copy = pltpu.make_async_copy(vir_hbm, vir_ref, small_sem.at[1])

    barrier = pltpu.get_barrier_semaphore()
    for bit in (1, 2, 4):
        pl.semaphore_signal(
            barrier, inc=1, device_id={"occ": flipped(me, bit)},
            device_id_type=pl.DeviceIdType.MESH,
        )

    @pl.loop(0, chunks)
    def _(q):
        local(q).start()

    energy_copy.start()
    vir_copy.start()
    pl.semaphore_wait(barrier, 3)

    def send(label, q, bit, send_sem):
        place = blocks.at[flipped(me, label), rows_of(q)]
        return pltpu.make_async_remote_copy(
            src_ref=place,
            dst_ref=place,
            send_sem=send_sem,
            recv_sem=recv_sem.at[flipped(label, bit), q],
            device_id={"occ": flipped(me, bit)},
            device_id_type=pl.DeviceIdType.MESH,
        )

    def own_send(q, axis):
        return send(0, q, 2 + 2 * axis, own_sem.at[axis, q])

    def far_send(q, label):
        return send(label, q, 6 - label, fwd_sem.at[q])

    def sib_send(q, label):
        return send(label, q, 1, sib_sem.at[label // 2, q])

    def arrived(label, q):
        place = blocks.at[flipped(me, label), rows_of(q)]
        pltpu.make_async_copy(place, place, recv_sem.at[label, q]).wait()

    def give(n):
        return pltpu.make_async_remote_copy(
            src_ref=held_a.at[n],
            dst_ref=held_b.at[n],
            send_sem=give_sem.at[n],
            recv_sem=take_sem.at[n],
            device_id={"occ": flipped(me, 1)},
            device_id_type=pl.DeviceIdType.MESH,
        )

    def taken(n):
        place = held_b.at[n]
        pltpu.make_async_copy(place, place, take_sem.at[n]).wait()

    def next_sends(q):
        @pl.when(q < chunks)
        def _():
            own_send(q, 0).start()
            own_send(q, 1).start()

        @pl.when(q >= chunks)
        def _():
            far_send(2 * (q - chunks), 2).start()
            far_send(2 * (q - chunks) + 1, 4).start()

    for q in range(DEPTH):
        local(q).wait()
        own_send(q, 0).start()
        own_send(q, 1).start()
        sib_send(q, 0).start()

    @pl.loop(DEPTH, chunks)
    def _(q):
        local(q).wait()
        sib_send(q, 0).start()

    energy_copy.wait()
    vir_copy.wait()
    total[...] = jnp.zeros_like(total)
    column = lax.broadcasted_iota(jnp.int32, (width, window), 1)
    row = lax.broadcasted_iota(jnp.int32, (width, window), 0)
    pick[...] = jnp.where(column == row + skip, 1.0, 0.0).astype(jnp.bfloat16)
    for t in range(steps):
        part = vir_ref[:, t * ROWS:(t + 1) * ROWS]
        vcol[t * ROWS:(t + 1) * ROWS, :] = jnp.broadcast_to(part, (ROWS, ROWS)).T

    def rows_at(t):
        return pl.ds(pl.multiple_of(t * ROWS, ROWS), ROWS)

    def turn_all(label):
        u = flipped(me, label)
        slabs[u] = lax.dot_general(
            pick[...], blocks[u, :, pl.ds(lead, window)], (((1,), (1,)), ((), ())),
            preferred_element_type=jnp.float32,
        ).astype(jnp.bfloat16)

    def turn(la, lb, t):
        ua, ub = flipped(me, la), flipped(me, lb)
        both = jnp.concatenate(
            [blocks[ua, rows_at(t), pl.ds(lead, window)], blocks[ub, rows_at(t), pl.ds(lead, window)]],
            axis=0,
        )
        moved = lax.dot_general(
            pick[...], both, (((1,), (1,)), ((), ())), preferred_element_type=jnp.float32
        ).astype(jnp.bfloat16)
        slabs[ua, :, rows_at(t)] = moved[:, :ROWS]
        slabs[ub, :, rows_at(t)] = moved[:, ROWS:]

    def amps_of(item, n):
        ua, ta, ub, tb, v = item
        some = jnp.concatenate([blocks[ua, rows_at(ta), :], blocks[ub, rows_at(tb), :]], axis=0)
        level = jnp.concatenate(
            [energy_ref[ua] - vir_ref[:, rows_at(ta)], energy_ref[ub] - vir_ref[:, rows_at(tb)]],
            axis=1,
        ) + energy_ref[v]
        for h in range(2):
            rows = slice(h * half, (h + 1) * half)
            kmat = lax.dot_general(
                blocks[v, rows, :], some, (((1,), (1,)), ((), ())),
                preferred_element_type=jnp.float32,
            )
            held_a[n, rows, :] = (kmat / (level - vcol[rows, 0:1])).astype(jnp.bfloat16)

    def gather(item, held):
        ua, ta, ub, tb, v = item
        left = jnp.concatenate([slabs[ua, :, rows_at(ta)], slabs[ub, :, rows_at(tb)]], axis=1)
        both = jnp.dot(slabs[v], held[...], preferred_element_type=jnp.float32)
        other = lax.dot_general(
            left, held[...], (((1,), (1,)), ((), ())), preferred_element_type=jnp.float32
        )
        total[ua, :, rows_at(ta)] += both[:, :ROWS]
        total[ub, :, rows_at(tb)] += both[:, ROWS:]
        total[v] += other

    def gather_both(pair, n):
        gather(pair[0], held_a.at[n])
        gather(pair[1], held_b.at[n])

    def placed(item):
        return (
            flipped(me, item[0]), jnp.int32(item[1]), flipped(me, item[2]), jnp.int32(item[3]),
            flipped(me, item[4]),
        )

    def mirrored(item):
        return (flipped(item[0], 1), item[1], flipped(item[2], 1), item[3], flipped(item[4], 1))

    def crossed(u, ta, w, tb, v):
        item = placed((u, ta, w, tb, v))
        return item, mirrored(item)

    def shared(label):
        even = flipped(me, label) // 2 * 2
        def rows(p):
            return (even, 2 * p, even, 2 * p + 1, even + 1)
        return rows(parity), rows(1 - parity)

    def step(n, pair, queue):
        amps_of(pair[0], n)
        if len(queue) == LAG:
            gather_both(queue[0], n - LAG)
            queue = queue[1:]
        return queue + (pair,)

    def run(n, pair, queue):
        if not (isinstance(n, int) and n == 0):
            give(n - 1).start()
        if len(queue) == LAG:
            taken(n - LAG)
        return step(n, pair, queue)

    @pl.loop(0, chunks)
    def _(q):
        arrived(1, q)

    turn_all(0)
    turn_all(1)
    queue = run(0, shared(0), ())

    def near_event(t):
        for k in (0, 1):
            q = 2 * t + k
            arrived(2, q)
            arrived(4, q)
            next_sends(q + DEPTH)
            sib_send(q, 2).start()
            sib_send(q, 4).start()
        turn(2, 4, t)
        for k in (0, 1):
            arrived(3, 2 * t + k)
            arrived(5, 2 * t + k)
        turn(3, 5, t)

    def near_pair(c, t):
        return crossed(2 + 3 * c, t - c, 3 + 2 * c, t, 0)

    def near(t, carry):
        near_event(t)
        return lax.fori_loop(
            0, 1 + t % 2, lambda c, g: (g[0] + 1, run(g[0], near_pair(c, t), g[1])), carry
        )

    near_event(0)
    queue = run(1, near_pair(0, 0), queue)
    near_event(1)
    queue = run(2, near_pair(0, 1), queue)
    carry = (jnp.int32(LAG), queue)
    carry = (carry[0] + 1, run(carry[0], near_pair(1, 1), carry[1]))
    carry = lax.fori_loop(2, steps, near, carry)

    def side(m, carry):
        n, queue = carry
        u, t, v = entry(SIDE, 0, m), entry(SIDE, 1, m), entry(SIDE, 2, m)
        return n + 1, run(n, crossed(u, t, u, t + 1, v), queue)

    def own_side(m, carry):
        n, queue = carry
        return n + 1, run(n, shared(2 + 2 * m), queue)

    def far_event(t):
        for k in (0, 1):
            q = 2 * t + k
            arrived(6, q)
            sib_send(q, 6).start()

        @pl.when(chunks + t + DEPTH < chunks + chunks // 2)
        def _():
            next_sends(chunks + t + DEPTH)

    def far_rest(t):
        turn(6, 6, t)
        for k in (0, 1):
            arrived(7, 2 * t + k)
        turn(7, 7, t)

    def far_pair(c, t):
        odd = c // 2
        return crossed(6, t - odd, 7 - odd, t, 4 * (c % 2) + 3 * odd)

    def far(t, carry):
        far_event(t)
        carry = lax.fori_loop(0, (t + 1) % 2 + t % 2, lambda m, g: side(t, g), carry)
        far_rest(t)
        return lax.fori_loop(
            0, 2 + t % 2, lambda c, g: (g[0] + 1, run(g[0], far_pair(c, t), g[1])), carry
        )

    carry = lax.fori_loop(0, 2, own_side, carry)
    carry = lax.fori_loop(0, steps, far, carry)
    n, queue = carry
    queue = run(n, shared(6), queue)
    give(n).start()
    for k in range(LAG):
        taken(n + 1 - LAG + k)
        gather_both(queue[k], n + 1 - LAG + k)

    for u in range(count):
        for c in range(virtuals // LANES):
            wide[c, pl.ds(u, width, count), :] = total[u, :, c * LANES:(c + 1) * LANES]
    for c in range(virtuals // LANES):
        out_ref[:, c * LANES:(c + 1) * LANES] = wide[c].astype(jnp.bfloat16)

    @pl.loop(0, held_a.shape[0])
    def _(n):
        give(n).wait_send()

    @pl.loop(0, steps)
    def _(t):
        for k in (0, 1):
            q = 2 * t + k
            own_send(q, 0).wait_send()
            own_send(q, 1).wait_send()
            for label in (0, 2, 4, 6):
                sib_send(q, label).wait_send()
            far_send(q, 2 if k == 0 else 4).wait_send()


def gathered(factors, occ_energy, vir_energy, coeffs):
    _, virtuals, depth = factors.shape
    count = lax.axis_size("occ")
    width = depth // count
    window = max(
        -(-(d * width % LANES + width) // LANES) * LANES for d in range(count)
    )
    chunks = virtuals // CHUNK
    rounds = count * OFFSETS
    pair_flops = 2 * virtuals * virtuals * (depth + 2 * width)
    gamma = pl.pallas_call(
        gathered_kernel,
        out_shape=jax.ShapeDtypeStruct((count * width, virtuals), jnp.bfloat16),
        in_specs=[pl.BlockSpec(memory_space=pltpu.HBM)] * 3,
        out_specs=pl.BlockSpec(memory_space=pltpu.VMEM),
        scratch_shapes=[
            pltpu.VMEM((count, virtuals, depth), jnp.bfloat16),
            pltpu.VMEM((count, width, virtuals), jnp.bfloat16),
            pltpu.VMEM((count, width, virtuals), jnp.float32),
            pltpu.VMEM((virtuals // LANES, count * width, LANES), jnp.float32),
            pltpu.VMEM((width, window), jnp.bfloat16),
            pltpu.VMEM((virtuals, ROWS), jnp.float32),
            pltpu.VMEM((rounds, virtuals, 2 * ROWS), jnp.bfloat16),
            pltpu.VMEM((rounds, virtuals, 2 * ROWS), jnp.bfloat16),
            pltpu.SMEM((count,), jnp.float32),
            pltpu.VMEM((1, virtuals), jnp.float32),
            pltpu.SemaphoreType.DMA((chunks,)),
            pltpu.SemaphoreType.DMA((2,)),
            pltpu.SemaphoreType.DMA((2, chunks)),
            pltpu.SemaphoreType.DMA((chunks,)),
            pltpu.SemaphoreType.DMA((4, chunks)),
            pltpu.SemaphoreType.DMA((8, chunks)),
            pltpu.SemaphoreType.DMA((rounds,)),
            pltpu.SemaphoreType.DMA((rounds,)),
        ],
        compiler_params=pltpu.CompilerParams(
            collective_id=0, has_side_effects=True, vmem_limit_bytes=52 * 1024 * 1024
        ),
        cost_estimate=pl.CostEstimate(
            flops=count * OFFSETS * pair_flops, bytes_accessed=count * virtuals * depth * 2,
            transcendentals=0,
        ),
    )(factors[0], occ_energy, vir_energy[None])
    back = jnp.dot(gamma, coeffs.T, preferred_element_type=jnp.float32).astype(jnp.bfloat16)
    return back.reshape(width, count, coeffs.shape[0])


def fits(count, virtuals, depth):
    width = depth // count
    return (
        count == 8
        and count == 2 * OFFSETS + 2
        and virtuals == 4 * ROWS
        and depth % (LANES * 2) == 0
        and width % 32 == 0
    )


def either(factors, occ_energy, vir_energy, coeffs):
    if fits(lax.axis_size("occ"), factors.shape[1], factors.shape[2]):
        return gathered(factors, occ_energy, vir_energy, coeffs)
    return on_device(factors, occ_energy, vir_energy, coeffs)


def solution(mesh):
    return jax.shard_map(
        either,
        mesh=mesh,
        in_specs=(P(("frag", "occ"), None, None), P("frag"), P("frag"), P("frag", None)),
        out_specs=P("occ", "frag", None),
        check_vma=False,
    )
```

time: 78.2 us -> 67.7 us (0.87)
  Pallas kernels: 70.8 us -> 62.7 us
  local copies, waits for them, and re-layouts: 5.67 us -> 1.43 us
  matrix products: 1.55 us -> 3.05 us
    pallas_call x1, Pallas kernels: 70.8 us -> 62.7 us  [gathered(): pl.pallas_call(gathered_kernel, out_shape=jax.ShapeDtypeStruct((count * w...]
    convert_element_type x1 -> x0, local copies, waits for them, and re-layouts: 2.93 us -> none  [gathered(): jnp.einsum('ipa,ma->pim', gamma, coeffs, preferred_element_type=jnp.float32)]
    dot_general x1, matrix products: 1.55 us -> 3.05 us  [gathered(): jnp.dot(gamma, coeffs.T, preferred_element_type=jnp.float32)]
    unnamed x8 -> x6, local copies, waits for them, and re-layouts: 2.74 us -> 1.43 us
where the time goes in v1:
time: 67.7 us; the launch traced here: 67.2 us
  Pallas kernels  62.7 us (93%)
  matrix products  3.05 us (5%)
  local copies, waits for them, and re-layouts  1.43 us (2%)
    pallas_call x1, Pallas kernels, gathered(): pl.pallas_call(gathered_kernel, out_shape=jax.ShapeDtypeStruct((count * w...  62.7 us
    dot_general x1, matrix products, gathered(): jnp.dot(gamma, coeffs.T, preferred_element_type=jnp.float32)  3.05 us
    unnamed x6, local copies, waits for them, and re-layouts  1.43 us

profile of v1, /device:TPU:1, one launch (start us, length us, event | category | flops | bytes accessed | tf_op | source)
XLA Modules:
  0.0 67.2 jit_solution(16172064917828267244)
XLA Ops:
  0.0 0.0 copy-start
  0.0 0.0 copy-start.1
  0.0 0.8 %copy-done.1 = f32[512]{0:T(512)S(1)} copy-done((f32[512]{0:T(512)S(1)}, f32[512]{0:T(512)}, u32[]{:S(2)}) %copy-start.1) | copy-done | bytes 2072
  0.8 0.0 copy-start.2
  0.8 0.7 copy-done.2
  1.4 62.7 %shard_map.46 = bf16[1280,512]{1,0:T(8,128)(2,1)S(1)} custom-call(bf16[512,1280]{1,0:T(8,128)(2,1)} %bitcast.7, f32[8]{0:T(128)S(1)} %copy-done.2, f32[1,512]{1,0:T(1,128)S(1)} %bitcast.6), custom_call_target="tpu_custom_call" | custom-call | flops 20132659200 | bytes 10485760 | tf_op jit(solution)/shard_map/pallas_call | solution.py:390
  64.2 0.0 copy-done
  64.2 3.0 %fusion = bf16[160,8,1024]{2,1,0:T(8,128)(2,1)} fusion(bf16[1280,512]{1,0:T(8,128)(2,1)S(1)} %shard_map.46, bf16[1024,512]{1,0:T(8,128)(2,1)S(1)} %copy-done), kind=kOutput, calls=%fused_computation.1 | convolution fusion | flops 1343488000 | bytes 4980736 | tf_op jit(solution)/shard_map/dot_general | solution.py:423
Async XLA Ops:
  0.0 64.2 %copy-start = (bf16[1024,512]{1,0:T(8,128)(2,1)S(1)}, bf16[1024,512]{1,0:T(8,128)(2,1)}, u32[]{:S(2)}) copy-start(bf16[1024,512]{1,0:T(8,128)(2,1)} %param.7) | copy-start | bytes 3145732
  0.0 0.8 %copy-start.1 = (f32[512]{0:T(512)S(1)}, f32[512]{0:T(512)}, u32[]{:S(2)}) copy-start(f32[512]{0:T(512)} %param.6) | copy-start | bytes 6148
  0.8 0.7 copy-start.2

commit v2 on v1

--- a/solution.py
+++ b/solution.py
@@ -56,10 +56,26 @@
 ROWS = 128
 CHUNK = ROWS // 2
 
-LAG = 3
-DEPTH = 2
-
-SIDE = ((2, 0, 4), (2, 2, 4), (2, 0, 5), (2, 2, 5))
+BACK_STEPS = 2
+DEPTH = 3
+AHEAD = 1
+
+ITEMS = (
+    ((0, 0, 0, 1, 1, 1), (2, 0, 3, 0, 0, 0)),
+    ((2, 1, 3, 1, 0, 0), (5, 0, 5, 1, 0, 0)),
+    ((2, 2, 3, 2, 0, 0), (2, 3, 3, 3, 0, 0)),
+    ((5, 2, 5, 3, 0, 0), (2, 0, 2, 1, 3, 1)),
+    ((4, 0, 4, 1, 5, 1), (2, 0, 2, 1, 4, 0)),
+    ((6, 0, 7, 0, 0, 0), (6, 0, 7, 0, 4, 0)),
+    ((2, 2, 2, 3, 4, 0), (2, 0, 2, 1, 5, 0)),
+    ((6, 1, 7, 1, 0, 0), (6, 1, 7, 1, 4, 0)),
+    ((6, 0, 6, 1, 3, 0), (2, 2, 2, 3, 5, 0)),
+    ((6, 2, 7, 2, 0, 0), (6, 2, 7, 2, 4, 0)),
+    ((6, 3, 7, 3, 0, 0), (6, 3, 7, 3, 4, 0)),
+    ((6, 2, 6, 3, 3, 0), (6, 0, 6, 1, 7, 1)),
+)
+PASSED = (3, 5, 7, 9)
+FAR = (5, 7, 9, 10)
 
 
 def flipped(a, b):
@@ -67,9 +83,16 @@
     return bits[0] + bits[1] + bits[2]
 
 
-def entry(table, column, n):
-    packed = sum(row[column] << (3 * k) for k, row in enumerate(table))
-    return lax.shift_right_logical(jnp.int32(packed), jnp.int32(3) * n) % 8
+def octal(packed, n):
+    return lax.shift_right_logical(packed, jnp.int32(3) * n) % 8
+
+
+def pack(ua, ta, ub, tb, v):
+    return ua + 8 * ta + 64 * ub + 512 * tb + 4096 * v
+
+
+def unpack(code):
+    return tuple(octal(code, k) for k in range(5))
 
 
 def gathered_kernel(
@@ -86,6 +109,7 @@
     steps = virtuals // ROWS
     chunks = virtuals // CHUNK
     half = virtuals // 2
+    rounds = len(ITEMS)
     first = me * width
     lead = pl.multiple_of(first // LANES * LANES, LANES)
     skip = first % LANES
@@ -142,8 +166,8 @@
 
     def give(n):
         return pltpu.make_async_remote_copy(
-            src_ref=held_a.at[n],
-            dst_ref=held_b.at[n],
+            src_ref=held_a.at[n + 2 * AHEAD],
+            dst_ref=held_b.at[n + 2 * AHEAD],
             send_sem=give_sem.at[n],
             recv_sem=take_sem.at[n],
             device_id={"occ": flipped(me, 1)},
@@ -151,7 +175,7 @@
         )
 
     def taken(n):
-        place = held_b.at[n]
+        place = held_b.at[n + 2 * AHEAD]
         pltpu.make_async_copy(place, place, take_sem.at[n]).wait()
 
     def next_sends(q):
@@ -179,6 +203,9 @@
     energy_copy.wait()
     vir_copy.wait()
     total[...] = jnp.zeros_like(total)
+    for n in range(2 * AHEAD):
+        held_a[n] = jnp.zeros(held_a.shape[1:], held_a.dtype)
+        held_b[n] = jnp.zeros(held_b.shape[1:], held_b.dtype)
     column = lax.broadcasted_iota(jnp.int32, (width, window), 1)
     row = lax.broadcasted_iota(jnp.int32, (width, window), 0)
     pick[...] = jnp.where(column == row + skip, 1.0, 0.0).astype(jnp.bfloat16)
@@ -208,8 +235,8 @@
         slabs[ua, :, rows_at(t)] = moved[:, :ROWS]
         slabs[ub, :, rows_at(t)] = moved[:, ROWS:]
 
-    def amps_of(item, n):
-        ua, ta, ub, tb, v = item
+    def amps_of(code, n):
+        ua, ta, ub, tb, v = unpack(code)
         some = jnp.concatenate([blocks[ua, rows_at(ta), :], blocks[ub, rows_at(tb), :]], axis=0)
         level = jnp.concatenate(
             [energy_ref[ua] - vir_ref[:, rows_at(ta)], energy_ref[ub] - vir_ref[:, rows_at(tb)]],
@@ -223,8 +250,8 @@
             )
             held_a[n, rows, :] = (kmat / (level - vcol[rows, 0:1])).astype(jnp.bfloat16)
 
-    def gather(item, held):
-        ua, ta, ub, tb, v = item
+    def gather(code, held):
+        ua, ta, ub, tb, v = unpack(code)
         left = jnp.concatenate([slabs[ua, :, rows_at(ta)], slabs[ub, :, rows_at(tb)]], axis=1)
         both = jnp.dot(slabs[v], held[...], preferred_element_type=jnp.float32)
         other = lax.dot_general(
@@ -234,42 +261,39 @@
         total[ub, :, rows_at(tb)] += both[:, ROWS:]
         total[v] += other
 
-    def gather_both(pair, n):
-        gather(pair[0], held_a.at[n])
-        gather(pair[1], held_b.at[n])
-
-    def placed(item):
-        return (
-            flipped(me, item[0]), jnp.int32(item[1]), flipped(me, item[2]), jnp.int32(item[3]),
-            flipped(me, item[4]),
-        )
-
-    def mirrored(item):
-        return (flipped(item[0], 1), item[1], flipped(item[2], 1), item[3], flipped(item[4], 1))
-
-    def crossed(u, ta, w, tb, v):
-        item = placed((u, ta, w, tb, v))
-        return item, mirrored(item)
-
-    def shared(label):
-        even = flipped(me, label) // 2 * 2
-        def rows(p):
-            return (even, 2 * p, even, 2 * p + 1, even + 1)
-        return rows(parity), rows(1 - parity)
-
-    def step(n, pair, queue):
-        amps_of(pair[0], n)
-        if len(queue) == LAG:
-            gather_both(queue[0], n - LAG)
-            queue = queue[1:]
-        return queue + (pair,)
-
-    def run(n, pair, queue):
-        if not (isinstance(n, int) and n == 0):
-            give(n - 1).start()
-        if len(queue) == LAG:
-            taken(n - LAG)
-        return step(n, pair, queue)
+    def gather_all(codes, n):
+        gather(codes[0], held_a.at[n])
+        gather(codes[1], held_b.at[n])
+        gather(codes[2], held_a.at[n + 1])
+        gather(codes[3], held_b.at[n + 1])
+
+    place_of = jnp.int32(0)
+    for label in range(8):
+        place_of = place_of + flipped(me, label) * 8 ** label
+
+    def codes_of(j):
+        codes = []
+        for s in range(2):
+            packed = jnp.int32(0)
+            for k in range(rounds):
+                row = ITEMS[k][s]
+                packed = jnp.where(j == k, sum(x << (3 * c) for c, x in enumerate(row)), packed)
+            lu, ta, lw, tb, lv, same = (octal(packed, c) for c in range(6))
+            turned_by = same * parity
+            ua, ub, v = (
+                octal(place_of, x) for x in (lu + turned_by, lw + turned_by, lv - turned_by)
+            )
+            codes.append(pack(ua, ta + 2 * turned_by, ub, tb + 2 * turned_by, v))
+            swap = 1 - same
+            shift = 2 * same * (1 - 2 * parity)
+            codes.append(
+                pack(
+                    ua + swap * (1 - 2 * (ua % 2)), ta + 2 * turned_by + shift,
+                    ub + swap * (1 - 2 * (ub % 2)), tb + 2 * turned_by + shift,
+                    v + swap * (1 - 2 * (v % 2)),
+                )
+            )
+        return tuple(codes)
 
     @pl.loop(0, chunks)
     def _(q):
@@ -277,7 +301,6 @@
 
     turn_all(0)
     turn_all(1)
-    queue = run(0, shared(0), ())
 
     def near_event(t):
         for k in (0, 1):
@@ -293,33 +316,7 @@
             arrived(5, 2 * t + k)
         turn(3, 5, t)
 
-    def near_pair(c, t):
-        return crossed(2 + 3 * c, t - c, 3 + 2 * c, t, 0)
-
-    def near(t, carry):
-        near_event(t)
-        return lax.fori_loop(
-            0, 1 + t % 2, lambda c, g: (g[0] + 1, run(g[0], near_pair(c, t), g[1])), carry
-        )
-
-    near_event(0)
-    queue = run(1, near_pair(0, 0), queue)
-    near_event(1)
-    queue = run(2, near_pair(0, 1), queue)
-    carry = (jnp.int32(LAG), queue)
-    carry = (carry[0] + 1, run(carry[0], near_pair(1, 1), carry[1]))
-    carry = lax.fori_loop(2, steps, near, carry)
-
-    def side(m, carry):
-        n, queue = carry
-        u, t, v = entry(SIDE, 0, m), entry(SIDE, 1, m), entry(SIDE, 2, m)
-        return n + 1, run(n, crossed(u, t, u, t + 1, v), queue)
-
-    def own_side(m, carry):
-        n, queue = carry
-        return n + 1, run(n, shared(2 + 2 * m), queue)
-
-    def far_event(t):
+    def pass_far(t):
         for k in (0, 1):
             q = 2 * t + k
             arrived(6, q)
@@ -329,32 +326,53 @@
         def _():
             next_sends(chunks + t + DEPTH)
 
-    def far_rest(t):
-        turn(6, 6, t)
+    def far_event(t):
         for k in (0, 1):
             arrived(7, 2 * t + k)
-        turn(7, 7, t)
-
-    def far_pair(c, t):
-        odd = c // 2
-        return crossed(6, t - odd, 7 - odd, t, 4 * (c % 2) + 3 * odd)
-
-    def far(t, carry):
-        far_event(t)
-        carry = lax.fori_loop(0, (t + 1) % 2 + t % 2, lambda m, g: side(t, g), carry)
-        far_rest(t)
-        return lax.fori_loop(
-            0, 2 + t % 2, lambda c, g: (g[0] + 1, run(g[0], far_pair(c, t), g[1])), carry
-        )
-
-    carry = lax.fori_loop(0, 2, own_side, carry)
-    carry = lax.fori_loop(0, steps, far, carry)
-    n, queue = carry
-    queue = run(n, shared(6), queue)
-    give(n).start()
-    for k in range(LAG):
-        taken(n + 1 - LAG + k)
-        gather_both(queue[k], n + 1 - LAG + k)
+        turn(6, 7, t)
+
+    def at(table, j, event):
+        step = jnp.int32(-1)
+        for t, k in enumerate(table):
+            step = jnp.where(j == k, t, step)
+
+        @pl.when(step >= 0)
+        def _():
+            event(step)
+
+    def body(j, carry):
+        last, now = carry
+
+        @pl.when(j < 2)
+        def _():
+            near_event(j)
+
+        @pl.when(j == 2)
+        def _():
+            near_event(j)
+            near_event(j + 1)
+
+        at(FAR, j, far_event)
+        amps_of(now[0], 2 * j + 2 * AHEAD)
+        amps_of(now[2], 2 * j + 2 * AHEAD + 1)
+        give(2 * j).start()
+        give(2 * j + 1).start()
+        at(PASSED, j, pass_far)
+
+        @pl.when(j >= AHEAD)
+        def _():
+            taken(2 * j - 2 * AHEAD)
+            taken(2 * j - 2 * AHEAD + 1)
+
+        gather_all(last, 2 * j)
+        return now, codes_of(j + 1)
+
+    first_codes = codes_of(jnp.int32(0))
+    nothing = (first_codes[0],) * 4
+    last, _ = lax.fori_loop(0, rounds, body, (nothing, first_codes))
+    taken(2 * rounds - 2)
+    taken(2 * rounds - 1)
+    gather_all(last, 2 * rounds)
 
     for u in range(count):
         for c in range(virtuals // LANES):
@@ -362,7 +380,7 @@
     for c in range(virtuals // LANES):
         out_ref[:, c * LANES:(c + 1) * LANES] = wide[c].astype(jnp.bfloat16)
 
-    @pl.loop(0, held_a.shape[0])
+    @pl.loop(0, 2 * rounds)
     def _(n):
         give(n).wait_send()
 
@@ -375,6 +393,34 @@
             for label in (0, 2, 4, 6):
                 sib_send(q, label).wait_send()
             far_send(q, 2 if k == 0 else 4).wait_send()
+
+
+def back_kernel(gamma_ref, coeffs_ref, out_ref):
+    out_ref[...] = lax.dot_general(
+        gamma_ref[...], coeffs_ref[...], (((1,), (1,)), ((), ())),
+        preferred_element_type=jnp.float32,
+    ).astype(out_ref.dtype)
+
+
+def back_of(gamma, coeffs):
+    rows, virtuals = gamma.shape
+    atomic = coeffs.shape[0]
+    block = atomic // BACK_STEPS
+    return pl.pallas_call(
+        back_kernel,
+        grid=(BACK_STEPS,),
+        out_shape=jax.ShapeDtypeStruct((rows, atomic), jnp.bfloat16),
+        in_specs=[
+            pl.BlockSpec((rows, virtuals), lambda i: (0, 0)),
+            pl.BlockSpec((block, virtuals), lambda i: (i, 0)),
+        ],
+        out_specs=pl.BlockSpec((rows, block), lambda i: (0, i)),
+        compiler_params=pltpu.CompilerParams(vmem_limit_bytes=32 * 1024 * 1024),
+        cost_estimate=pl.CostEstimate(
+            flops=2 * rows * virtuals * atomic, transcendentals=0,
+            bytes_accessed=2 * (rows * virtuals + atomic * virtuals + rows * atomic),
+        ),
+    )(gamma, coeffs)
 
 
 def gathered(factors, occ_energy, vir_energy, coeffs):
@@ -399,8 +445,8 @@
             pltpu.VMEM((virtuals // LANES, count * width, LANES), jnp.float32),
             pltpu.VMEM((width, window), jnp.bfloat16),
             pltpu.VMEM((virtuals, ROWS), jnp.float32),
-            pltpu.VMEM((rounds, virtuals, 2 * ROWS), jnp.bfloat16),
-            pltpu.VMEM((rounds, virtuals, 2 * ROWS), jnp.bfloat16),
+            pltpu.VMEM((rounds + 2 * AHEAD, virtuals, 2 * ROWS), jnp.bfloat16),
+            pltpu.VMEM((rounds + 2 * AHEAD, virtuals, 2 * ROWS), jnp.bfloat16),
             pltpu.SMEM((count,), jnp.float32),
             pltpu.VMEM((1, virtuals), jnp.float32),
             pltpu.SemaphoreType.DMA((chunks,)),
@@ -413,14 +459,18 @@
             pltpu.SemaphoreType.DMA((rounds,)),
         ],
         compiler_params=pltpu.CompilerParams(
-            collective_id=0, has_side_effects=True, vmem_limit_bytes=52 * 1024 * 1024
+            collective_id=0, has_side_effects=True, vmem_limit_bytes=int(52 * 1024 * 1024)
         ),
         cost_estimate=pl.CostEstimate(
             flops=count * OFFSETS * pair_flops, bytes_accessed=count * virtuals * depth * 2,
             transcendentals=0,
         ),
-    )(factors[0], occ_energy, vir_energy[None])
-    back = jnp.dot(gamma, coeffs.T, preferred_element_type=jnp.float32).astype(jnp.bfloat16)
+    )(
+        factors[0],
+        pltpu.with_memory_space_constraint(occ_energy, pltpu.HBM),
+        pltpu.with_memory_space_constraint(vir_energy[None], pltpu.HBM),
+    )
+    back = back_of(gamma, coeffs)
     return back.reshape(width, count, coeffs.shape[0])
 
 
@@ -428,7 +478,7 @@
     width = depth // count
     return (
         count == 8
-        and count == 2 * OFFSETS + 2
+        and count * OFFSETS == 2 * len(ITEMS)
         and virtuals == 4 * ROWS
         and depth % (LANES * 2) == 0
         and width % 32 == 0

time: 67.7 us -> 62.1 us (0.917)
  matrix products: 3.05 us -> 0 us
  local copies, waits for them, and re-layouts: 1.43 us -> 0.01 us
  Pallas kernels: 62.7 us -> 61.7 us
    pallas_call x1, Pallas kernels: 62.7 us -> 58.9 us  [gathered(): pl.pallas_call(gathered_kernel, out_shape=jax.ShapeDtypeStruct((count * w...]
    dot_general x1 -> x0, matrix products: 3.05 us -> none  [gathered(): jnp.dot(gamma, coeffs.T, preferred_element_type=jnp.float32)]
    pallas_call x0 -> x1, Pallas kernels: none -> 2.85 us  [back_of(): pl.pallas_call(back_kernel, grid=(BACK_STEPS,), out_shape=jax.ShapeDtypeS...]
    unnamed x6 -> x2, local copies, waits for them, and re-layouts: 1.43 us -> 0.01 us
where the time goes in v2:
time: 62.1 us; the launch traced here: 61.8 us
  Pallas kernels  61.7 us (99%)
    pallas_call x1, Pallas kernels, gathered(): pl.pallas_call(gathered_kernel, out_shape=jax.ShapeDtypeStruct((count * w...  58.9 us
    pallas_call x1, Pallas kernels, back_of(): pl.pallas_call(back_kernel, grid=(BACK_STEPS,), out_shape=jax.ShapeDtypeS...  2.85 us

profile of v2, /device:TPU:1, one launch (start us, length us, event | category | flops | bytes accessed | tf_op | source)
XLA Modules:
  0.0 61.8 jit_solution(1748577721685408181)
XLA Ops:
  0.0 0.0 copy-start
  0.0 58.9 %shard_map.46.gamma_ref = bf16[1280,512]{1,0:T(8,128)(2,1)S(1)} custom-call(bf16[512,1280]{1,0:T(8,128)(2,1)} %bitcast.3, f32[8]{0:T(128)} %energy_hbm.1, f32[1,512]{1,0:T(1,128)} %bitcast.4), custom_call_target="tpu_custom_call" | custom-call | flops 20132659200 | bytes 10485760 | tf_op jit(solution)/shard_map/pallas_call | solution.py:436
  58.9 0.0 copy-done
  58.9 2.9 %shard_map.47 = bf16[1280,1024]{1,0:T(8,128)(2,1)} custom-call(bf16[1280,512]{1,0:T(8,128)(2,1)S(1)} %shard_map.46.gamma_ref, bf16[1024,512]{1,0:T(8,128)(2,1)S(1)} %copy-done), custom_call_target="tpu_custom_call" | custom-call | flops 1342177280 | bytes 4980736 | tf_op jit(solution)/shard_map/pallas_call | solution.py:409
Async XLA Ops:
  0.0 58.9 %copy-start = (bf16[1024,512]{1,0:T(8,128)(2,1)S(1)}, bf16[1024,512]{1,0:T(8,128)(2,1)}, u32[]{:S(2)}) copy-start(bf16[1024,512]{1,0:T(8,128)(2,1)} %coeffs_ref.1) | copy-start | bytes 3145732

commit v3 on v2

--- a/solution.py
+++ b/solution.py
@@ -56,26 +56,26 @@
 ROWS = 128
 CHUNK = ROWS // 2
 
-BACK_STEPS = 2
+BACK_STEPS = 4
 DEPTH = 3
-AHEAD = 1
 
 ITEMS = (
-    ((0, 0, 0, 1, 1, 1), (2, 0, 3, 0, 0, 0)),
-    ((2, 1, 3, 1, 0, 0), (5, 0, 5, 1, 0, 0)),
-    ((2, 2, 3, 2, 0, 0), (2, 3, 3, 3, 0, 0)),
-    ((5, 2, 5, 3, 0, 0), (2, 0, 2, 1, 3, 1)),
-    ((4, 0, 4, 1, 5, 1), (2, 0, 2, 1, 4, 0)),
+    ((0, 0, 0, 1, 1, 1), (0, 0, 0, 1, 1, 1)),
+    ((2, 0, 3, 0, 0, 0), (2, 1, 3, 1, 0, 0)),
+    ((5, 0, 5, 1, 0, 0), (2, 2, 3, 2, 0, 0)),
+    ((2, 3, 3, 3, 0, 0), (5, 2, 5, 3, 0, 0)),
+    ((2, 0, 2, 1, 3, 1), (4, 0, 4, 1, 5, 1)),
+    ((2, 0, 2, 1, 4, 0), (2, 2, 2, 3, 4, 0)),
     ((6, 0, 7, 0, 0, 0), (6, 0, 7, 0, 4, 0)),
-    ((2, 2, 2, 3, 4, 0), (2, 0, 2, 1, 5, 0)),
+    ((2, 0, 2, 1, 5, 0), (2, 2, 2, 3, 5, 0)),
     ((6, 1, 7, 1, 0, 0), (6, 1, 7, 1, 4, 0)),
-    ((6, 0, 6, 1, 3, 0), (2, 2, 2, 3, 5, 0)),
     ((6, 2, 7, 2, 0, 0), (6, 2, 7, 2, 4, 0)),
+    ((6, 0, 6, 1, 3, 0), (6, 2, 6, 3, 3, 0)),
     ((6, 3, 7, 3, 0, 0), (6, 3, 7, 3, 4, 0)),
-    ((6, 2, 6, 3, 3, 0), (6, 0, 6, 1, 7, 1)),
+    ((6, 0, 6, 1, 7, 1), (6, 0, 6, 1, 7, 1)),
 )
-PASSED = (3, 5, 7, 9)
-FAR = (5, 7, 9, 10)
+PASSED = (4, 6, 7, 9)
+FAR = (6, 8, 9, 11)
 
 
 def flipped(a, b):
@@ -166,8 +166,8 @@
 
     def give(n):
         return pltpu.make_async_remote_copy(
-            src_ref=held_a.at[n + 2 * AHEAD],
-            dst_ref=held_b.at[n + 2 * AHEAD],
+            src_ref=held_a.at[n],
+            dst_ref=held_b.at[n],
             send_sem=give_sem.at[n],
             recv_sem=take_sem.at[n],
             device_id={"occ": flipped(me, 1)},
@@ -175,7 +175,7 @@
         )
 
     def taken(n):
-        place = held_b.at[n + 2 * AHEAD]
+        place = held_b.at[n]
         pltpu.make_async_copy(place, place, take_sem.at[n]).wait()
 
     def next_sends(q):
@@ -203,7 +203,7 @@
     energy_copy.wait()
     vir_copy.wait()
     total[...] = jnp.zeros_like(total)
-    for n in range(2 * AHEAD):
+    for n in range(3):
         held_a[n] = jnp.zeros(held_a.shape[1:], held_a.dtype)
         held_b[n] = jnp.zeros(held_b.shape[1:], held_b.dtype)
     column = lax.broadcasted_iota(jnp.int32, (width, window), 1)
@@ -341,38 +341,50 @@
             event(step)
 
     def body(j, carry):
-        last, now = carry
-
-        @pl.when(j < 2)
+        last, mid, now = carry
+
+        @pl.when(j == 1)
+        def _():
+            near_event(0)
+
+        @pl.when(j <= 3)
         def _():
             near_event(j)
 
-        @pl.when(j == 2)
-        def _():
-            near_event(j)
-            near_event(j + 1)
-
         at(FAR, j, far_event)
-        amps_of(now[0], 2 * j + 2 * AHEAD)
-        amps_of(now[2], 2 * j + 2 * AHEAD + 1)
-        give(2 * j).start()
-        give(2 * j + 1).start()
+        amps_of(now[0], 2 * j + 2)
+        amps_of(now[2], 2 * j + 3)
+        give(2 * j + 2).start()
+        give(2 * j + 3).start()
         at(PASSED, j, pass_far)
 
-        @pl.when(j >= AHEAD)
-        def _():
-            taken(2 * j - 2 * AHEAD)
-            taken(2 * j - 2 * AHEAD + 1)
-
-        gather_all(last, 2 * j)
-        return now, codes_of(j + 1)
-
-    first_codes = codes_of(jnp.int32(0))
-    nothing = (first_codes[0],) * 4
-    last, _ = lax.fori_loop(0, rounds, body, (nothing, first_codes))
-    taken(2 * rounds - 2)
-    taken(2 * rounds - 1)
-    gather_all(last, 2 * rounds)
+        @pl.when(j >= 2)
+        def _():
+            taken(2 * j - 1)
+
+        @pl.when(j >= 3)
+        def _():
+            taken(2 * j - 2)
+
+        gather_all(last, 2 * j - 2)
+        return mid, now, codes_of(j + 1)
+
+    front = codes_of(jnp.int32(0))
+    amps_of(front[2], 3)
+    give(3).start()
+    final = rounds - 1
+    last, mid, now = lax.fori_loop(1, final, body, (front, front, codes_of(jnp.int32(1))))
+    amps_of(now[0], 2 * final + 2)
+    give(2 * final + 2).start()
+    taken(2 * final - 2)
+    taken(2 * final - 1)
+    gather_all(last, 2 * final - 2)
+    taken(2 * final)
+    taken(2 * final + 1)
+    gather_all(mid, 2 * final)
+    gather(now[0], held_a.at[2 * final + 2])
+    taken(2 * final + 2)
+    gather(now[1], held_b.at[2 * final + 2])
 
     for u in range(count):
         for c in range(virtuals // LANES):
@@ -380,7 +392,7 @@
     for c in range(virtuals // LANES):
         out_ref[:, c * LANES:(c + 1) * LANES] = wide[c].astype(jnp.bfloat16)
 
-    @pl.loop(0, 2 * rounds)
+    @pl.loop(3, 2 * rounds + 1)
     def _(n):
         give(n).wait_send()
 
@@ -395,26 +407,36 @@
             far_send(q, 2 if k == 0 else 4).wait_send()
 
 
-def back_kernel(gamma_ref, coeffs_ref, out_ref):
-    out_ref[...] = lax.dot_general(
-        gamma_ref[...], coeffs_ref[...], (((1,), (1,)), ((), ())),
-        preferred_element_type=jnp.float32,
-    ).astype(out_ref.dtype)
+def back_kernel(gamma_ref, coeffs_ref, out_ref, done, done_sem):
+    block = done.shape[1]
+
+    def put(i):
+        return pltpu.make_async_copy(
+            done.at[i], out_ref.at[pl.ds(i * block, block)], done_sem.at[i]
+        )
+
+    for i in range(BACK_STEPS):
+        done[i] = lax.dot_general(
+            gamma_ref[i * block:(i + 1) * block, :], coeffs_ref[...], (((1,), (1,)), ((), ())),
+            preferred_element_type=jnp.float32,
+        ).astype(done.dtype)
+        put(i).start()
+    for i in range(BACK_STEPS):
+        put(i).wait()
 
 
 def back_of(gamma, coeffs):
     rows, virtuals = gamma.shape
     atomic = coeffs.shape[0]
-    block = atomic // BACK_STEPS
     return pl.pallas_call(
         back_kernel,
-        grid=(BACK_STEPS,),
         out_shape=jax.ShapeDtypeStruct((rows, atomic), jnp.bfloat16),
-        in_specs=[
-            pl.BlockSpec((rows, virtuals), lambda i: (0, 0)),
-            pl.BlockSpec((block, virtuals), lambda i: (i, 0)),
+        in_specs=[pl.BlockSpec(memory_space=pltpu.VMEM)] * 2,
+        out_specs=pl.BlockSpec(memory_space=pltpu.HBM),
+        scratch_shapes=[
+            pltpu.VMEM((BACK_STEPS, rows // BACK_STEPS, atomic), jnp.bfloat16),
+            pltpu.SemaphoreType.DMA((BACK_STEPS,)),
         ],
-        out_specs=pl.BlockSpec((rows, block), lambda i: (0, i)),
         compiler_params=pltpu.CompilerParams(vmem_limit_bytes=32 * 1024 * 1024),
         cost_estimate=pl.CostEstimate(
             flops=2 * rows * virtuals * atomic, transcendentals=0,
@@ -431,7 +453,6 @@
         -(-(d * width % LANES + width) // LANES) * LANES for d in range(count)
     )
     chunks = virtuals // CHUNK
-    rounds = count * OFFSETS
     pair_flops = 2 * virtuals * virtuals * (depth + 2 * width)
     gamma = pl.pallas_call(
         gathered_kernel,
@@ -445,8 +466,8 @@
             pltpu.VMEM((virtuals // LANES, count * width, LANES), jnp.float32),
             pltpu.VMEM((width, window), jnp.bfloat16),
             pltpu.VMEM((virtuals, ROWS), jnp.float32),
-            pltpu.VMEM((rounds + 2 * AHEAD, virtuals, 2 * ROWS), jnp.bfloat16),
-            pltpu.VMEM((rounds + 2 * AHEAD, virtuals, 2 * ROWS), jnp.bfloat16),
+            pltpu.VMEM((2 * len(ITEMS) + 1, virtuals, 2 * ROWS), jnp.bfloat16),
+            pltpu.VMEM((2 * len(ITEMS) + 1, virtuals, 2 * ROWS), jnp.bfloat16),
             pltpu.SMEM((count,), jnp.float32),
             pltpu.VMEM((1, virtuals), jnp.float32),
             pltpu.SemaphoreType.DMA((chunks,)),
@@ -455,8 +476,8 @@
             pltpu.SemaphoreType.DMA((chunks,)),
             pltpu.SemaphoreType.DMA((4, chunks)),
             pltpu.SemaphoreType.DMA((8, chunks)),
-            pltpu.SemaphoreType.DMA((rounds,)),
-            pltpu.SemaphoreType.DMA((rounds,)),
+            pltpu.SemaphoreType.DMA((2 * len(ITEMS) + 1,)),
+            pltpu.SemaphoreType.DMA((2 * len(ITEMS) + 1,)),
         ],
         compiler_params=pltpu.CompilerParams(
             collective_id=0, has_side_effects=True, vmem_limit_bytes=int(52 * 1024 * 1024)
@@ -478,7 +499,7 @@
     width = depth // count
     return (
         count == 8
-        and count * OFFSETS == 2 * len(ITEMS)
+        and count * OFFSETS == 2 * len(ITEMS) - 2
         and virtuals == 4 * ROWS
         and depth % (LANES * 2) == 0
         and width % 32 == 0

time: 62.1 us -> 60.6 us (0.976)
  Pallas kernels: 61.7 us -> 59.9 us
    pallas_call x1, Pallas kernels: 58.9 us -> 57.5 us  [gathered(): pl.pallas_call(gathered_kernel, out_shape=jax.ShapeDtypeStruct((count * w...]
where the time goes in v3:
time: 60.6 us; the launch traced here: 59.9 us
  Pallas kernels  59.9 us (99%)
    pallas_call x1, Pallas kernels, gathered(): pl.pallas_call(gathered_kernel, out_shape=jax.ShapeDtypeStruct((count * w...  57.5 us
    pallas_call x1, Pallas kernels, back_of(): pl.pallas_call(back_kernel, out_shape=jax.ShapeDtypeStruct((rows, atomic)...  2.43 us

profile of v3, /device:TPU:1, one launch (start us, length us, event | category | flops | bytes accessed | tf_op | source)
XLA Modules:
  0.0 59.9 jit_solution(12185665685753550596)
XLA Ops:
  0.0 0.0 copy-start
  0.0 57.5 %shard_map.46.gamma_ref = bf16[1280,512]{1,0:T(8,128)(2,1)S(1)} custom-call(bf16[512,1280]{1,0:T(8,128)(2,1)} %bitcast.3, f32[8]{0:T(128)} %energy_hbm.1, f32[1,512]{1,0:T(1,128)} %bitcast.4), custom_call_target="tpu_custom_call" | custom-call | flops 20132659200 | bytes 10485760 | tf_op jit(solution)/shard_map/pallas_call | solution.py:457
  57.5 0.0 copy-done
  57.5 2.4 %shard_map.47 = bf16[1280,1024]{1,0:T(8,128)(2,1)} custom-call(bf16[1280,512]{1,0:T(8,128)(2,1)S(1)} %shard_map.46.gamma_ref, bf16[1024,512]{1,0:T(8,128)(2,1)S(1)} %copy-done), custom_call_target="tpu_custom_call" | custom-call | flops 1342177280 | bytes 4980736 | tf_op jit(solution)/shard_map/pallas_call | solution.py:431
Async XLA Ops:
  0.0 57.5 %copy-start = (bf16[1024,512]{1,0:T(8,128)(2,1)S(1)}, bf16[1024,512]{1,0:T(8,128)(2,1)}, u32[]{:S(2)}) copy-start(bf16[1024,512]{1,0:T(8,128)(2,1)} %coeffs_ref.1) | copy-start | bytes 3145732

commit v4 on v3

--- a/solution.py
+++ b/solution.py
@@ -63,9 +63,9 @@
     ((0, 0, 0, 1, 1, 1), (0, 0, 0, 1, 1, 1)),
     ((2, 0, 3, 0, 0, 0), (2, 1, 3, 1, 0, 0)),
     ((5, 0, 5, 1, 0, 0), (2, 2, 3, 2, 0, 0)),
+    ((2, 0, 2, 1, 4, 0), (2, 2, 2, 3, 4, 0)),
+    ((2, 0, 2, 1, 3, 1), (4, 0, 4, 1, 5, 1)),
     ((2, 3, 3, 3, 0, 0), (5, 2, 5, 3, 0, 0)),
-    ((2, 0, 2, 1, 3, 1), (4, 0, 4, 1, 5, 1)),
-    ((2, 0, 2, 1, 4, 0), (2, 2, 2, 3, 4, 0)),
     ((6, 0, 7, 0, 0, 0), (6, 0, 7, 0, 4, 0)),
     ((2, 0, 2, 1, 5, 0), (2, 2, 2, 3, 5, 0)),
     ((6, 1, 7, 1, 0, 0), (6, 1, 7, 1, 4, 0)),
@@ -74,7 +74,7 @@
     ((6, 3, 7, 3, 0, 0), (6, 3, 7, 3, 4, 0)),
     ((6, 0, 6, 1, 7, 1), (6, 0, 6, 1, 7, 1)),
 )
-PASSED = (4, 6, 7, 9)
+PASSED = (4, 6, 8, 9)
 FAR = (6, 8, 9, 11)
 
 
@@ -302,7 +302,7 @@
     turn_all(0)
     turn_all(1)
 
-    def near_event(t):
+    def near_pass(t):
         for k in (0, 1):
             q = 2 * t + k
             arrived(2, q)
@@ -310,6 +310,8 @@
             next_sends(q + DEPTH)
             sib_send(q, 2).start()
             sib_send(q, 4).start()
+
+    def near_take(t):
         turn(2, 4, t)
         for k in (0, 1):
             arrived(3, 2 * t + k)
@@ -345,11 +347,16 @@
 
         @pl.when(j == 1)
         def _():
-            near_event(0)
-
-        @pl.when(j <= 3)
-        def _():
-            near_event(j)
+            near_pass(0)
+            near_take(0)
+
+        @pl.when(j <= steps - 1)
+        def _():
+            near_pass(j)
+
+        @pl.when((j <= steps - 2) | (j == steps))
+        def _():
+            near_take(j - j // steps)
 
         at(FAR, j, far_event)
         amps_of(now[0], 2 * j + 2)
@@ -383,12 +390,18 @@
     taken(2 * final + 1)
     gather_all(mid, 2 * final)
     gather(now[0], held_a.at[2 * final + 2])
+
+    def spread(label):
+        u = flipped(me, label)
+        for c in range(virtuals // LANES):
+            wide[c, pl.ds(u, width, count), :] = total[u, :, c * LANES:(c + 1) * LANES]
+
+    for label in range(6):
+        spread(label)
     taken(2 * final + 2)
     gather(now[1], held_b.at[2 * final + 2])
-
-    for u in range(count):
-        for c in range(virtuals // LANES):
-            wide[c, pl.ds(u, width, count), :] = total[u, :, c * LANES:(c + 1) * LANES]
+    for label in (6, 7):
+        spread(label)
     for c in range(virtuals // LANES):
         out_ref[:, c * LANES:(c + 1) * LANES] = wide[c].astype(jnp.bfloat16)
 

time: 60.6 us -> 60.1 us (level)
  no operation moved by 1% of the time
where the time goes in v4:
time: 60.1 us; the launch traced here: 59.9 us
  Pallas kernels  59.9 us (100%)
    pallas_call x1, Pallas kernels, gathered(): pl.pallas_call(gathered_kernel, out_shape=jax.ShapeDtypeStruct((count * w...  57.5 us
    pallas_call x1, Pallas kernels, back_of(): pl.pallas_call(back_kernel, out_shape=jax.ShapeDtypeStruct((rows, atomic)...  2.43 us

profile of v4, /device:TPU:1, one launch (start us, length us, event | category | flops | bytes accessed | tf_op | source)
XLA Modules:
  0.0 59.9 jit_solution(16703453370580278686)
XLA Ops:
  0.0 0.0 copy-start
  0.0 57.5 %shard_map.46.gamma_ref = bf16[1280,512]{1,0:T(8,128)(2,1)S(1)} custom-call(bf16[512,1280]{1,0:T(8,128)(2,1)} %bitcast.3, f32[8]{0:T(128)} %energy_hbm.1, f32[1,512]{1,0:T(1,128)} %bitcast.4), custom_call_target="tpu_custom_call" | custom-call | flops 20132659200 | bytes 10485760 | tf_op jit(solution)/shard_map/pallas_call | solution.py:470
  57.5 0.0 copy-done
  57.5 2.4 %shard_map.47 = bf16[1280,1024]{1,0:T(8,128)(2,1)} custom-call(bf16[1280,512]{1,0:T(8,128)(2,1)S(1)} %shard_map.46.gamma_ref, bf16[1024,512]{1,0:T(8,128)(2,1)S(1)} %copy-done), custom_call_target="tpu_custom_call" | custom-call | flops 1342177280 | bytes 4980736 | tf_op jit(solution)/shard_map/pallas_call | solution.py:444
Async XLA Ops:
  0.0 57.5 %copy-start = (bf16[1024,512]{1,0:T(8,128)(2,1)S(1)}, bf16[1024,512]{1,0:T(8,128)(2,1)}, u32[]{:S(2)}) copy-start(bf16[1024,512]{1,0:T(8,128)(2,1)} %coeffs_ref.1) | copy-start | bytes 3145732

commit v5 on v4

--- a/solution.py
+++ b/solution.py
@@ -56,7 +56,7 @@
 ROWS = 128
 CHUNK = ROWS // 2
 
-BACK_STEPS = 4
+BACK_STEPS = 2
 DEPTH = 3
 
 ITEMS = (

time: 60.1 us -> 60.3 us (level)
  no operation moved by 1% of the time
where the time goes in v5:
time: 60.3 us; the launch traced here: 60.1 us
  Pallas kernels  60.1 us (100%)
    pallas_call x1, Pallas kernels, gathered(): pl.pallas_call(gathered_kernel, out_shape=jax.ShapeDtypeStruct((count * w...  57.5 us
    pallas_call x1, Pallas kernels, back_of(): pl.pallas_call(back_kernel, out_shape=jax.ShapeDtypeStruct((rows, atomic)...  2.63 us

profile of v5, /device:TPU:1, one launch (start us, length us, event | category | flops | bytes accessed | tf_op | source)
XLA Modules:
  0.0 60.1 jit_solution(12844089904539277303)
XLA Ops:
  0.0 0.0 copy-start
  0.0 57.5 %shard_map.46.gamma_ref = bf16[1280,512]{1,0:T(8,128)(2,1)S(1)} custom-call(bf16[512,1280]{1,0:T(8,128)(2,1)} %bitcast.3, f32[8]{0:T(128)} %energy_hbm.1, f32[1,512]{1,0:T(1,128)} %bitcast.4), custom_call_target="tpu_custom_call" | custom-call | flops 20132659200 | bytes 10485760 | tf_op jit(solution)/shard_map/pallas_call | solution.py:470
  57.5 0.0 copy-done
  57.5 2.6 %shard_map.47 = bf16[1280,1024]{1,0:T(8,128)(2,1)} custom-call(bf16[1280,512]{1,0:T(8,128)(2,1)S(1)} %shard_map.46.gamma_ref, bf16[1024,512]{1,0:T(8,128)(2,1)S(1)} %copy-done), custom_call_target="tpu_custom_call" | custom-call | flops 1342177280 | bytes 4980736 | tf_op jit(solution)/shard_map/pallas_call | solution.py:444
Async XLA Ops:
  0.0 57.5 %copy-start = (bf16[1024,512]{1,0:T(8,128)(2,1)S(1)}, bf16[1024,512]{1,0:T(8,128)(2,1)}, u32[]{:S(2)}) copy-start(bf16[1024,512]{1,0:T(8,128)(2,1)} %coeffs_ref.1) | copy-start | bytes 3145732
